TPU v7x, 512 devices: a 8x2x16 block of a 8x16x16 slice. The times are simulated.
512 devices in a mesh: parts: 2 (over y), blk: 16 (over z), sub: 8 (over x), rep: 2 (over core).
Axes of the slice: x: 8, y: 2, z: 16, core: 2. Of those that a mesh axis runs over, the one named last changes fastest.
The devices are a block of a 8x16x16 slice.
Arguments:
- queries: bfloat16 [2048, 32, 128], P(('parts', 'blk', 'sub', 'rep')), parts along dimension 0, may hold values from -1.5 to 1.5
- passages: bfloat16 [2048, 128, 128], P(('parts', 'blk')), parts along dimension 0, may hold values from -1.5 to 1.5
- lengths: int32 [2048], P(('parts', 'blk')), parts along dimension 0, may hold values from 8 to 128
- slot_of: int32 [2048], P('parts'), parts along dimension 0, may hold values from 0 to 1023, each once
- candidates: int32 [2048, 256], P(('parts', 'blk', 'sub', 'rep')), parts along dimension 0, may hold values from 0 to 1023
Outputs:
- score: float32 [2048, 256], P(('parts', 'blk', 'sub', 'rep')), parts along dimension 0
- top: float32 [2048, 10], P(('parts', 'blk', 'sub', 'rep')), parts along dimension 0
There are 2 independent parts, one for each index of `parts`. A program takes and returns all parts, laid end to end along the dimension named above; each array names one. Nothing has to cross between parts.
Inputs may be any that keep to these rules, and one draw needn't show every extreme that they name: `slot_of`: a permutation; storage row r lies on the blk index r // 64. `candidates`: passage ids, repeats allowed. `lengths`: the live slots of a row are its first ones.
All inputs are finite; a program needn't handle non-finite values.
Results may differ from a plain program's by a relative error of at most 0.0003.
Values may be sent and summed in bfloat16 or wider, within the bound.
A program may use at most 64 MiB of HBM per device.

v0:
```python
import jax
import jax.numpy as jnp
from jax import lax
from jax.sharding import PartitionSpec as P

TOPN = 10


def score_table(rows_q, passages, lengths):
    queries_here = rows_q.shape[0]
    tokens = rows_q.shape[1]
    width = rows_q.shape[2]
    count = passages.shape[0]
    span = passages.shape[1]
    group = 4
    flat = rows_q.reshape(queries_here * tokens, width)
    blocks = passages.reshape(count // group, group * span, width)
    spans = lengths.reshape(count // group, group)

    def one_block(pair):
        piece, live_count = pair
        similar = lax.dot_general(
            flat, piece, (((1,), (1,)), ((), ())), preferred_element_type=jnp.float32
        )
        similar = similar.reshape(queries_here * tokens, group, span)
        live = lax.broadcasted_iota(jnp.int32, (group, span), 1) < live_count[:, None]
        best = jnp.max(jnp.where(live[None], similar, -1e30), axis=2)
        return jnp.sum(best.reshape(queries_here, tokens, group), axis=1) / tokens

    table = lax.map(one_block, (blocks, spans))
    return jnp.transpose(table, (1, 0, 2)).reshape(queries_here, count)


def shards(queries, passages, lengths, slot_of, candidates):
    table = score_table(lax.all_gather(queries, "blk", axis=0, tiled=True), passages, lengths)
    whole = lax.all_to_all(table, "blk", split_axis=0, concat_axis=1, tiled=True)
    score = jnp.take_along_axis(whole, jnp.take(slot_of, candidates, axis=0), axis=1)
    top = lax.top_k(score, TOPN)[0]
    return (score, top)


def solution(mesh):
    return jax.shard_map(
        shards,
        mesh=mesh,
        in_specs=(
            P(("parts", "blk", "sub", "rep"), None, None),
            P(("parts", "blk"), None, None),
            P(("parts", "blk")),
            P("parts"),
            P(("parts", "blk", "sub", "rep"), None),
        ),
        out_specs=(
            P(("parts", "blk", "sub", "rep"), None),
            P(("parts", "blk", "sub", "rep"), None),
        ),
        check_vma=False,
    )
```

profile of v0, /device:TPU:86, one launch (start us, length us, event | category | flops | bytes accessed | tf_op | source)
XLA Modules:
  0.0 134.1 jit_solution(3773919563160055687)
XLA Ops:
  0.7 0.7 reshape.67
  1.4 71.3 %all_gather.3 = bf16[64,32,128]{2,1,0:T(8,128)(2,1)S(1)} all-gather(bf16[4,32,128]{2,1,0:T(8,128)(2,1)} %param.7), channel_id=1, replica_groups=mesh['parts'=2,'blk'=16,'sub'=8,'rep'=2] {'blk'}, dimensions={0}, use_global_device_ids=true | all-gather | bytes 557056 | tf_op jit(solution)/shard_map/all_gather | solution.py:35
  72.6 31.7 %while.10 = (s32[]{:T(128)}, f32[16,64,4]{1,2,0:T(4,128)S(1)}, s32[16,4]{1,0:T(8,128)S(1)}, bf16[16,512,128]{2,1,0:T(8,128)(2,1)}, bf16[2048,128]{1,0:T(8,128)(2,1)S(1)}, /*index=5*/s32[]{:T(128)}, f32[]{:T(128)}) while((s32[]{:T(128)}, f32[16,64,4]{1,2,0:T(4,128)S(1)}, s32[16,4]{1,0:T(8,128)S(1)}, bf16[16,512,128]{2,1,0:T(8,128)(2,1)}, ...), condition=%wide.region_3.4_spmd, body=%wide.region_0.3_spmd.sunk | while | flops 270533120 | bytes 792725 | solution.py:30
  72.7 0.1 iota_compare_fusion.2
  72.7 1.7 %select_reduce_fusion.2 = f32[2048,4]{0,1:T(4,128)S(1)} fusion(pred[4,128]{1,0:T(4,128)(4,1)S(1)} %iota_compare_fusion.2, bf16[2048,128]{1,0:T(8,128)(2,1)S(1)} %get-tuple-element.93, bf16[16,512,128]{2,1,0:T(8,128)(2,1)} %get-tuple-element.92, s32[]{:T(128)S(6)} %copy.19), kind=kOutput, calls=%fused_computation.2.clone.1 | convolution fusion | flops 270524416 | bytes 688644 | tf_op jit(solution)/shard_map/while/body/eval_jaxpr/dot_general | solution.py:22
  74.4 0.1 reshape.95
  74.5 0.1 reduce_sum.10
  74.7 1.6 %select_reduce_fusion.2 = f32[2048,4]{0,1:T(4,128)S(1)} fusion(pred[4,128]{1,0:T(4,128)(4,1)S(1)} %iota_compare_fusion.2, bf16[2048,128]{1,0:T(8,128)(2,1)S(1)} %get-tuple-element.93, bf16[16,512,128]{2,1,0:T(8,128)(2,1)} %get-tuple-element.92, s32[]{:T(128)S(6)} %copy.19), kind=kOutput, calls=%fused_computation.2.clone.1 | convolution fusion | flops 270524416 | bytes 688644 | tf_op jit(solution)/shard_map/while/body/eval_jaxpr/dot_general | solution.py:22
  76.4 0.1 reshape.95
  76.5 0.1 reduce_sum.10
  76.7 1.6 %select_reduce_fusion.2 = f32[2048,4]{0,1:T(4,128)S(1)} fusion(pred[4,128]{1,0:T(4,128)(4,1)S(1)} %iota_compare_fusion.2, bf16[2048,128]{1,0:T(8,128)(2,1)S(1)} %get-tuple-element.93, bf16[16,512,128]{2,1,0:T(8,128)(2,1)} %get-tuple-element.92, s32[]{:T(128)S(6)} %copy.19), kind=kOutput, calls=%fused_computation.2.clone.1 | convolution fusion | flops 270524416 | bytes 688644 | tf_op jit(solution)/shard_map/while/body/eval_jaxpr/dot_general | solution.py:22
  78.3 0.1 reshape.95
  78.4 0.1 reduce_sum.10
  78.7 1.6 %select_reduce_fusion.2 = f32[2048,4]{0,1:T(4,128)S(1)} fusion(pred[4,128]{1,0:T(4,128)(4,1)S(1)} %iota_compare_fusion.2, bf16[2048,128]{1,0:T(8,128)(2,1)S(1)} %get-tuple-element.93, bf16[16,512,128]{2,1,0:T(8,128)(2,1)} %get-tuple-element.92, s32[]{:T(128)S(6)} %copy.19), kind=kOutput, calls=%fused_computation.2.clone.1 | convolution fusion | flops 270524416 | bytes 688644 | tf_op jit(solution)/shard_map/while/body/eval_jaxpr/dot_general | solution.py:22
  80.3 0.1 reshape.95
  80.4 0.1 reduce_sum.10
  80.7 1.6 %select_reduce_fusion.2 = f32[2048,4]{0,1:T(4,128)S(1)} fusion(pred[4,128]{1,0:T(4,128)(4,1)S(1)} %iota_compare_fusion.2, bf16[2048,128]{1,0:T(8,128)(2,1)S(1)} %get-tuple-element.93, bf16[16,512,128]{2,1,0:T(8,128)(2,1)} %get-tuple-element.92, s32[]{:T(128)S(6)} %copy.19), kind=kOutput, calls=%fused_computation.2.clone.1 | convolution fusion | flops 270524416 | bytes 688644 | tf_op jit(solution)/shard_map/while/body/eval_jaxpr/dot_general | solution.py:22
  82.3 0.1 reshape.95
  82.4 0.1 reduce_sum.10
  82.6 1.6 %select_reduce_fusion.2 = f32[2048,4]{0,1:T(4,128)S(1)} fusion(pred[4,128]{1,0:T(4,128)(4,1)S(1)} %iota_compare_fusion.2, bf16[2048,128]{1,0:T(8,128)(2,1)S(1)} %get-tuple-element.93, bf16[16,512,128]{2,1,0:T(8,128)(2,1)} %get-tuple-element.92, s32[]{:T(128)S(6)} %copy.19), kind=kOutput, calls=%fused_computation.2.clone.1 | convolution fusion | flops 270524416 | bytes 688644 | tf_op jit(solution)/shard_map/while/body/eval_jaxpr/dot_general | solution.py:22
  84.3 0.1 reshape.95
  84.4 0.1 reduce_sum.10
  84.6 1.6 %select_reduce_fusion.2 = f32[2048,4]{0,1:T(4,128)S(1)} fusion(pred[4,128]{1,0:T(4,128)(4,1)S(1)} %iota_compare_fusion.2, bf16[2048,128]{1,0:T(8,128)(2,1)S(1)} %get-tuple-element.93, bf16[16,512,128]{2,1,0:T(8,128)(2,1)} %get-tuple-element.92, s32[]{:T(128)S(6)} %copy.19), kind=kOutput, calls=%fused_computation.2.clone.1 | convolution fusion | flops 270524416 | bytes 688644 | tf_op jit(solution)/shard_map/while/body/eval_jaxpr/dot_general | solution.py:22
  86.3 0.1 reshape.95
  86.4 0.1 reduce_sum.10
  86.6 1.6 %select_reduce_fusion.2 = f32[2048,4]{0,1:T(4,128)S(1)} fusion(pred[4,128]{1,0:T(4,128)(4,1)S(1)} %iota_compare_fusion.2, bf16[2048,128]{1,0:T(8,128)(2,1)S(1)} %get-tuple-element.93, bf16[16,512,128]{2,1,0:T(8,128)(2,1)} %get-tuple-element.92, s32[]{:T(128)S(6)} %copy.19), kind=kOutput, calls=%fused_computation.2.clone.1 | convolution fusion | flops 270524416 | bytes 688644 | tf_op jit(solution)/shard_map/while/body/eval_jaxpr/dot_general | solution.py:22
  88.2 0.1 reshape.95
  88.3 0.1 reduce_sum.10
  88.6 1.6 %select_reduce_fusion.2 = f32[2048,4]{0,1:T(4,128)S(1)} fusion(pred[4,128]{1,0:T(4,128)(4,1)S(1)} %iota_compare_fusion.2, bf16[2048,128]{1,0:T(8,128)(2,1)S(1)} %get-tuple-element.93, bf16[16,512,128]{2,1,0:T(8,128)(2,1)} %get-tuple-element.92, s32[]{:T(128)S(6)} %copy.19), kind=kOutput, calls=%fused_computation.2.clone.1 | convolution fusion | flops 270524416 | bytes 688644 | tf_op jit(solution)/shard_map/while/body/eval_jaxpr/dot_general | solution.py:22
  90.2 0.1 reshape.95
  90.3 0.1 reduce_sum.10
  90.6 1.6 %select_reduce_fusion.2 = f32[2048,4]{0,1:T(4,128)S(1)} fusion(pred[4,128]{1,0:T(4,128)(4,1)S(1)} %iota_compare_fusion.2, bf16[2048,128]{1,0:T(8,128)(2,1)S(1)} %get-tuple-element.93, bf16[16,512,128]{2,1,0:T(8,128)(2,1)} %get-tuple-element.92, s32[]{:T(128)S(6)} %copy.19), kind=kOutput, calls=%fused_computation.2.clone.1 | convolution fusion | flops 270524416 | bytes 688644 | tf_op jit(solution)/shard_map/while/body/eval_jaxpr/dot_general | solution.py:22
  92.2 0.1 reshape.95
  92.3 0.1 reduce_sum.10
  92.5 1.6 %select_reduce_fusion.2 = f32[2048,4]{0,1:T(4,128)S(1)} fusion(pred[4,128]{1,0:T(4,128)(4,1)S(1)} %iota_compare_fusion.2, bf16[2048,128]{1,0:T(8,128)(2,1)S(1)} %get-tuple-element.93, bf16[16,512,128]{2,1,0:T(8,128)(2,1)} %get-tuple-element.92, s32[]{:T(128)S(6)} %copy.19), kind=kOutput, calls=%fused_computation.2.clone.1 | convolution fusion | flops 270524416 | bytes 688644 | tf_op jit(solution)/shard_map/while/body/eval_jaxpr/dot_general | solution.py:22
  94.2 0.1 reshape.95
  94.3 0.1 reduce_sum.10
  94.5 1.6 %select_reduce_fusion.2 = f32[2048,4]{0,1:T(4,128)S(1)} fusion(pred[4,128]{1,0:T(4,128)(4,1)S(1)} %iota_compare_fusion.2, bf16[2048,128]{1,0:T(8,128)(2,1)S(1)} %get-tuple-element.93, bf16[16,512,128]{2,1,0:T(8,128)(2,1)} %get-tuple-element.92, s32[]{:T(128)S(6)} %copy.19), kind=kOutput, calls=%fused_computation.2.clone.1 | convolution fusion | flops 270524416 | bytes 688644 | tf_op jit(solution)/shard_map/while/body/eval_jaxpr/dot_general | solution.py:22
  96.2 0.1 reshape.95
  96.3 0.1 reduce_sum.10
  96.5 1.6 %select_reduce_fusion.2 = f32[2048,4]{0,1:T(4,128)S(1)} fusion(pred[4,128]{1,0:T(4,128)(4,1)S(1)} %iota_compare_fusion.2, bf16[2048,128]{1,0:T(8,128)(2,1)S(1)} %get-tuple-element.93, bf16[16,512,128]{2,1,0:T(8,128)(2,1)} %get-tuple-element.92, s32[]{:T(128)S(6)} %copy.19), kind=kOutput, calls=%fused_computation.2.clone.1 | convolution fusion | flops 270524416 | bytes 688644 | tf_op jit(solution)/shard_map/while/body/eval_jaxpr/dot_general | solution.py:22
  98.1 0.1 reshape.95
  98.2 0.1 reduce_sum.10
  98.5 1.6 %select_reduce_fusion.2 = f32[2048,4]{0,1:T(4,128)S(1)} fusion(pred[4,128]{1,0:T(4,128)(4,1)S(1)} %iota_compare_fusion.2, bf16[2048,128]{1,0:T(8,128)(2,1)S(1)} %get-tuple-element.93, bf16[16,512,128]{2,1,0:T(8,128)(2,1)} %get-tuple-element.92, s32[]{:T(128)S(6)} %copy.19), kind=kOutput, calls=%fused_computation.2.clone.1 | convolution fusion | flops 270524416 | bytes 688644 | tf_op jit(solution)/shard_map/while/body/eval_jaxpr/dot_general | solution.py:22
  100.1 0.1 reshape.95
  100.2 0.1 reduce_sum.10
  100.5 1.6 %select_reduce_fusion.2 = f32[2048,4]{0,1:T(4,128)S(1)} fusion(pred[4,128]{1,0:T(4,128)(4,1)S(1)} %iota_compare_fusion.2, bf16[2048,128]{1,0:T(8,128)(2,1)S(1)} %get-tuple-element.93, bf16[16,512,128]{2,1,0:T(8,128)(2,1)} %get-tuple-element.92, s32[]{:T(128)S(6)} %copy.19), kind=kOutput, calls=%fused_computation.2.clone.1 | convolution fusion | flops 270524416 | bytes 688644 | tf_op jit(solution)/shard_map/while/body/eval_jaxpr/dot_general | solution.py:22
  102.1 0.1 reshape.95
  102.2 0.1 reduce_sum.10
  102.4 1.6 %select_reduce_fusion.2 = f32[2048,4]{0,1:T(4,128)S(1)} fusion(pred[4,128]{1,0:T(4,128)(4,1)S(1)} %iota_compare_fusion.2, bf16[2048,128]{1,0:T(8,128)(2,1)S(1)} %get-tuple-element.93, bf16[16,512,128]{2,1,0:T(8,128)(2,1)} %get-tuple-element.92, s32[]{:T(128)S(6)} %copy.19), kind=kOutput, calls=%fused_computation.2.clone.1 | convolution fusion | flops 270524416 | bytes 688644 | tf_op jit(solution)/shard_map/while/body/eval_jaxpr/dot_general | solution.py:22
  104.1 0.1 reshape.95
  104.2 0.1 reduce_sum.10
  104.3 0.3 reshape.91
  104.6 0.3 copy.13
  104.9 0.7 reshape.92
  105.6 3.9 %all-to-all-start = ((f32[16,1,256]{2,1,0:T(1,128)}), f32[16,1,256]{2,1,0:T(1,128)S(1)}, u32[]{:S(2)}, u32[]{:S(2)}) async-start(f32[16,1,256]{2,1,0:T(1,128)} %reshape.92), calls=%async_computation | async-start | bytes 32768 | tf_op jit(solution)/shard_map/all_to_all | solution.py:36
  109.6 4.5 %gather_fusion = s32[1024]{0:T(1024)S(1)} fusion(s32[1024]{0:T(1024)S(1)} %copy-done, s32[1024]{0:T(1024)S(1)} %broadcast_clamp_fusion), kind=kCustom, calls=%fused_computation | custom fusion | bytes 12288 | tf_op jit(solution)/shard_map/jit(_take)/gather | solution.py:37
  114.2 7.5 %all-to-all-done = f32[16,1,256]{2,1,0:T(1,128)S(1)} async-done(((f32[16,1,256]{2,1,0:T(1,128)}), f32[16,1,256]{2,1,0:T(1,128)S(1)}, u32[]{:S(2)}, u32[]{:S(2)}) %all-to-all-start) | async-done | bytes 16416 | tf_op jit(solution)/shard_map/all_to_all | solution.py:36
  121.6 0.5 broadcast.70
  122.2 0.7 reduce
  122.8 0.1 reshape.93
  122.9 0.1 all_to_all.17
  123.0 9.1 %gather_fusion.1 = f32[1024]{0:T(1024)S(1)} fusion(f32[4,1024]{1,0:T(4,128)S(1)} %all_to_all.17, s32[1024]{0:T(1024)S(1)} %bitcast.43), kind=kCustom, calls=%fused_computation.1 | custom fusion | bytes 16384 | tf_op jit(solution)/shard_map/jit(take_along_axis)/gather | solution.py:37
  132.2 1.9 %sort_prefixfusion = f32[4,10]{1,0:T(4,128)} fusion(f32[4,256]{1,0:T(4,128)S(1)} %and_select_fusion), kind=kCustom, calls=%top_k.9.sort_prefix | custom fusion | flops 10240 | bytes 4256 | tf_op jit(solution)/shard_map/top_k | solution.py:38
  (63 shorter events, 1.6 us)
Async XLA Ops:
  0.6 109.0 %copy-start = (s32[1024]{0:T(1024)S(1)}, s32[1024]{0:T(1024)}, u32[]{:S(2)}) copy-start(s32[1024]{0:T(1024)} %param.10) | copy-start | bytes 12292
  72.6 36.9 %copy-start.1 = (s32[4,256]{1,0:T(4,128)S(1)}, s32[4,256]{1,0:T(4,128)}, u32[]{:S(2)}) copy-start(s32[4,256]{1,0:T(4,128)} %param.11) | copy-start | bytes 12292
  105.6 16.0 %all-to-all-start = ((f32[16,1,256]{2,1,0:T(1,128)}), f32[16,1,256]{2,1,0:T(1,128)S(1)}, u32[]{:S(2)}, u32[]{:S(2)}) async-start(f32[16,1,256]{2,1,0:T(1,128)} %reshape.92), calls=%async_computation | async-start | bytes 32768 | tf_op jit(solution)/shard_map/all_to_all | solution.py:36
  132.2 1.9 %copy-start.2 = (f32[4,256]{1,0:T(4,128)}, f32[4,256]{1,0:T(4,128)S(1)}, u32[]{:S(2)}) copy-start(f32[4,256]{1,0:T(4,128)S(1)} %and_select_fusion) | copy-start | bytes 12292
where the time goes:
time: 135 us; the launch traced here: 134 us
  blocking collectives  71.3 us (53%)
  matrix products  26.2 us (19%)
  local copies, waits for them, and re-layouts  18.1 us (13%)
  waiting for transfers between devices  7.45 us (6%)
  other arithmetic  5.8 us (4%)
  starting transfers between devices  3.93 us (3%)
    all_gather x1, blocking collectives, shards(): lax.all_gather(queries, 'blk', axis=0, tiled=True)  71.3 us
    dot_general x16, matrix products, one_block(): lax.dot_general(flat, piece, (((1,), (1,)), ((), ())), preferred_element_...  26.2 us
    gather x2, local copies, waits for them, and re-layouts, shards(): jnp.take_along_axis(whole, jnp.take(slot_of, candidates, axis=0), axis=1)  9.13 us
    all_to_all x1, waiting for transfers between devices, shards(): lax.all_to_all(table, 'blk', split_axis=0, concat_axis=1, tiled=True)  7.45 us
    gather x2, local copies, waits for them, and re-layouts, shards(): jnp.take(slot_of, candidates, axis=0)  4.54 us
    all_to_all x1, starting transfers between devices, shards(): lax.all_to_all(table, 'blk', split_axis=0, concat_axis=1, tiled=True)  3.93 us
  transfers between devices with their start and end apart: 1, of which 1 were waited for; matrix products, arithmetic and copies ran while one was open for 3% of the time, Pallas kernels for 0%

commit v1 on v0

--- a/solution.py
+++ b/solution.py
@@ -33,7 +33,10 @@
 
 def shards(queries, passages, lengths, slot_of, candidates):
     table = score_table(lax.all_gather(queries, "blk", axis=0, tiled=True), passages, lengths)
-    whole = lax.all_to_all(table, "blk", split_axis=0, concat_axis=1, tiled=True)
+    whole = jnp.concatenate(
+        lax.all_to_all(jnp.stack(jnp.split(table, lax.axis_size("blk"), axis=0)), "blk", 0, 0),
+        axis=1,
+    )
     score = jnp.take_along_axis(whole, jnp.take(slot_of, candidates, axis=0), axis=1)
     top = lax.top_k(score, TOPN)[0]
     return (score, top)

time: 135 us -> 134 us (level)
  the two profiles are of different devices: /device:TPU:86 before, /device:TPU:92 now
where the time goes in v1:
time: 134 us
  blocking collectives  71.3 us (53%)
  matrix products  26.2 us (20%)
  local copies, waits for them, and re-layouts  17.5 us (13%)
  waiting for transfers between devices  7.45 us (6%)
  other arithmetic  5.8 us (4%)
  starting transfers between devices  3.93 us (3%)
    all_gather x1, blocking collectives, shards(): lax.all_gather(queries, 'blk', axis=0, tiled=True)  71.3 us
    dot_general x16, matrix products, one_block(): lax.dot_general(flat, piece, (((1,), (1,)), ((), ())), preferred_element_...  26.2 us
    all_to_all x1, waiting for transfers between devices, shards(): lax.all_to_all(jnp.stack(jnp.split(table, lax.axis_size('blk'), axis=0)),...  7.45 us
    gather x2, local copies, waits for them, and re-layouts, shards(): jnp.take_along_axis(whole, jnp.take(slot_of, candidates, axis=0), axis=1)  7.3 us
    gather x2, local copies, waits for them, and re-layouts, shards(): jnp.take(slot_of, candidates, axis=0)  4.54 us
    all_to_all x1, starting transfers between devices, shards(): lax.all_to_all(jnp.stack(jnp.split(table, lax.axis_size('blk'), axis=0)),...  3.93 us
  transfers between devices with their start and end apart: 1, of which 1 were waited for; matrix products, arithmetic and copies ran while one was open for 3% of the time, Pallas kernels for 0%

profile of v1, /device:TPU:92, one launch (start us, length us, event | category | flops | bytes accessed | tf_op | source)
XLA Modules:
  0.0 133.7 jit_solution(17445397237092499851)
XLA Ops:
  0.7 71.3 %all_gather.3 = bf16[64,32,128]{2,1,0:T(8,128)(2,1)S(1)} all-gather(bf16[4,32,128]{2,1,0:T(8,128)(2,1)} %param.7), channel_id=1, replica_groups=mesh['parts'=2,'blk'=16,'sub'=8,'rep'=2] {'blk'}, dimensions={0}, use_global_device_ids=true | all-gather | bytes 557056 | tf_op jit(solution)/shard_map/all_gather | solution.py:35
  71.9 0.7 reshape.101
  72.7 31.7 %while.10 = (s32[]{:T(128)}, f32[16,64,4]{1,2,0:T(4,128)S(1)}, s32[16,4]{1,0:T(8,128)S(1)}, bf16[16,512,128]{2,1,0:T(8,128)(2,1)}, bf16[2048,128]{1,0:T(8,128)(2,1)S(1)}, /*index=5*/s32[]{:T(128)}, f32[]{:T(128)}) while((s32[]{:T(128)}, f32[16,64,4]{1,2,0:T(4,128)S(1)}, s32[16,4]{1,0:T(8,128)S(1)}, bf16[16,512,128]{2,1,0:T(8,128)(2,1)}, ...), condition=%wide.region_3.4_spmd, body=%wide.region_0.3_spmd.sunk | while | flops 270533120 | bytes 793225 | solution.py:30
  72.7 0.1 iota_compare_fusion.2
  72.8 1.6 %select_reduce_fusion.2 = f32[2048,4]{0,1:T(4,128)S(1)} fusion(pred[4,128]{1,0:T(4,128)(4,1)S(1)} %iota_compare_fusion.2, bf16[2048,128]{1,0:T(8,128)(2,1)S(1)} %get-tuple-element.109, bf16[16,512,128]{2,1,0:T(8,128)(2,1)} %get-tuple-element.108, s32[]{:T(128)} %get-tuple-element.98), kind=kOutput, calls=%fused_computation.2.clone.1 | convolution fusion | flops 270524416 | bytes 689152 | tf_op jit(solution)/shard_map/while/body/eval_jaxpr/dot_general | solution.py:22
  74.4 0.1 reshape.130
  74.5 0.1 reduce_sum.10
  74.7 0.1 iota_compare_fusion.2
  74.8 1.6 %select_reduce_fusion.2 = f32[2048,4]{0,1:T(4,128)S(1)} fusion(pred[4,128]{1,0:T(4,128)(4,1)S(1)} %iota_compare_fusion.2, bf16[2048,128]{1,0:T(8,128)(2,1)S(1)} %get-tuple-element.109, bf16[16,512,128]{2,1,0:T(8,128)(2,1)} %get-tuple-element.108, s32[]{:T(128)} %get-tuple-element.98), kind=kOutput, calls=%fused_computation.2.clone.1 | convolution fusion | flops 270524416 | bytes 689152 | tf_op jit(solution)/shard_map/while/body/eval_jaxpr/dot_general | solution.py:22
  76.4 0.1 reshape.130
  76.5 0.1 reduce_sum.10
  76.8 1.6 %select_reduce_fusion.2 = f32[2048,4]{0,1:T(4,128)S(1)} fusion(pred[4,128]{1,0:T(4,128)(4,1)S(1)} %iota_compare_fusion.2, bf16[2048,128]{1,0:T(8,128)(2,1)S(1)} %get-tuple-element.109, bf16[16,512,128]{2,1,0:T(8,128)(2,1)} %get-tuple-element.108, s32[]{:T(128)} %get-tuple-element.98), kind=kOutput, calls=%fused_computation.2.clone.1 | convolution fusion | flops 270524416 | bytes 689152 | tf_op jit(solution)/shard_map/while/body/eval_jaxpr/dot_general | solution.py:22
  78.4 0.1 reshape.130
  78.5 0.1 reduce_sum.10
  78.7 1.6 %select_reduce_fusion.2 = f32[2048,4]{0,1:T(4,128)S(1)} fusion(pred[4,128]{1,0:T(4,128)(4,1)S(1)} %iota_compare_fusion.2, bf16[2048,128]{1,0:T(8,128)(2,1)S(1)} %get-tuple-element.109, bf16[16,512,128]{2,1,0:T(8,128)(2,1)} %get-tuple-element.108, s32[]{:T(128)} %get-tuple-element.98), kind=kOutput, calls=%fused_computation.2.clone.1 | convolution fusion | flops 270524416 | bytes 689152 | tf_op jit(solution)/shard_map/while/body/eval_jaxpr/dot_general | solution.py:22
  80.4 0.1 reshape.130
  80.5 0.1 reduce_sum.10
  80.7 1.6 %select_reduce_fusion.2 = f32[2048,4]{0,1:T(4,128)S(1)} fusion(pred[4,128]{1,0:T(4,128)(4,1)S(1)} %iota_compare_fusion.2, bf16[2048,128]{1,0:T(8,128)(2,1)S(1)} %get-tuple-element.109, bf16[16,512,128]{2,1,0:T(8,128)(2,1)} %get-tuple-element.108, s32[]{:T(128)} %get-tuple-element.98), kind=kOutput, calls=%fused_computation.2.clone.1 | convolution fusion | flops 270524416 | bytes 689152 | tf_op jit(solution)/shard_map/while/body/eval_jaxpr/dot_general | solution.py:22
  82.4 0.1 reshape.130
  82.5 0.1 reduce_sum.10
  82.7 1.6 %select_reduce_fusion.2 = f32[2048,4]{0,1:T(4,128)S(1)} fusion(pred[4,128]{1,0:T(4,128)(4,1)S(1)} %iota_compare_fusion.2, bf16[2048,128]{1,0:T(8,128)(2,1)S(1)} %get-tuple-element.109, bf16[16,512,128]{2,1,0:T(8,128)(2,1)} %get-tuple-element.108, s32[]{:T(128)} %get-tuple-element.98), kind=kOutput, calls=%fused_computation.2.clone.1 | convolution fusion | flops 270524416 | bytes 689152 | tf_op jit(solution)/shard_map/while/body/eval_jaxpr/dot_general | solution.py:22
  84.3 0.1 reshape.130
  84.4 0.1 reduce_sum.10
  84.7 1.6 %select_reduce_fusion.2 = f32[2048,4]{0,1:T(4,128)S(1)} fusion(pred[4,128]{1,0:T(4,128)(4,1)S(1)} %iota_compare_fusion.2, bf16[2048,128]{1,0:T(8,128)(2,1)S(1)} %get-tuple-element.109, bf16[16,512,128]{2,1,0:T(8,128)(2,1)} %get-tuple-element.108, s32[]{:T(128)} %get-tuple-element.98), kind=kOutput, calls=%fused_computation.2.clone.1 | convolution fusion | flops 270524416 | bytes 689152 | tf_op jit(solution)/shard_map/while/body/eval_jaxpr/dot_general | solution.py:22
  86.3 0.1 reshape.130
  86.4 0.1 reduce_sum.10
  86.7 1.6 %select_reduce_fusion.2 = f32[2048,4]{0,1:T(4,128)S(1)} fusion(pred[4,128]{1,0:T(4,128)(4,1)S(1)} %iota_compare_fusion.2, bf16[2048,128]{1,0:T(8,128)(2,1)S(1)} %get-tuple-element.109, bf16[16,512,128]{2,1,0:T(8,128)(2,1)} %get-tuple-element.108, s32[]{:T(128)} %get-tuple-element.98), kind=kOutput, calls=%fused_computation.2.clone.1 | convolution fusion | flops 270524416 | bytes 689152 | tf_op jit(solution)/shard_map/while/body/eval_jaxpr/dot_general | solution.py:22
  88.3 0.1 reshape.130
  88.4 0.1 reduce_sum.10
  88.6 1.6 %select_reduce_fusion.2 = f32[2048,4]{0,1:T(4,128)S(1)} fusion(pred[4,128]{1,0:T(4,128)(4,1)S(1)} %iota_compare_fusion.2, bf16[2048,128]{1,0:T(8,128)(2,1)S(1)} %get-tuple-element.109, bf16[16,512,128]{2,1,0:T(8,128)(2,1)} %get-tuple-element.108, s32[]{:T(128)} %get-tuple-element.98), kind=kOutput, calls=%fused_computation.2.clone.1 | convolution fusion | flops 270524416 | bytes 689152 | tf_op jit(solution)/shard_map/while/body/eval_jaxpr/dot_general | solution.py:22
  90.3 0.1 reshape.130
  90.4 0.1 reduce_sum.10
  90.6 1.6 %select_reduce_fusion.2 = f32[2048,4]{0,1:T(4,128)S(1)} fusion(pred[4,128]{1,0:T(4,128)(4,1)S(1)} %iota_compare_fusion.2, bf16[2048,128]{1,0:T(8,128)(2,1)S(1)} %get-tuple-element.109, bf16[16,512,128]{2,1,0:T(8,128)(2,1)} %get-tuple-element.108, s32[]{:T(128)} %get-tuple-element.98), kind=kOutput, calls=%fused_computation.2.clone.1 | convolution fusion | flops 270524416 | bytes 689152 | tf_op jit(solution)/shard_map/while/body/eval_jaxpr/dot_general | solution.py:22
  92.3 0.1 reshape.130
  92.4 0.1 reduce_sum.10
  92.6 1.6 %select_reduce_fusion.2 = f32[2048,4]{0,1:T(4,128)S(1)} fusion(pred[4,128]{1,0:T(4,128)(4,1)S(1)} %iota_compare_fusion.2, bf16[2048,128]{1,0:T(8,128)(2,1)S(1)} %get-tuple-element.109, bf16[16,512,128]{2,1,0:T(8,128)(2,1)} %get-tuple-element.108, s32[]{:T(128)} %get-tuple-element.98), kind=kOutput, calls=%fused_computation.2.clone.1 | convolution fusion | flops 270524416 | bytes 689152 | tf_op jit(solution)/shard_map/while/body/eval_jaxpr/dot_general | solution.py:22
  94.2 0.1 reshape.130
  94.3 0.1 reduce_sum.10
  94.6 1.6 %select_reduce_fusion.2 = f32[2048,4]{0,1:T(4,128)S(1)} fusion(pred[4,128]{1,0:T(4,128)(4,1)S(1)} %iota_compare_fusion.2, bf16[2048,128]{1,0:T(8,128)(2,1)S(1)} %get-tuple-element.109, bf16[16,512,128]{2,1,0:T(8,128)(2,1)} %get-tuple-element.108, s32[]{:T(128)} %get-tuple-element.98), kind=kOutput, calls=%fused_computation.2.clone.1 | convolution fusion | flops 270524416 | bytes 689152 | tf_op jit(solution)/shard_map/while/body/eval_jaxpr/dot_general | solution.py:22
  96.2 0.1 reshape.130
  96.3 0.1 reduce_sum.10
  96.5 1.6 %select_reduce_fusion.2 = f32[2048,4]{0,1:T(4,128)S(1)} fusion(pred[4,128]{1,0:T(4,128)(4,1)S(1)} %iota_compare_fusion.2, bf16[2048,128]{1,0:T(8,128)(2,1)S(1)} %get-tuple-element.109, bf16[16,512,128]{2,1,0:T(8,128)(2,1)} %get-tuple-element.108, s32[]{:T(128)} %get-tuple-element.98), kind=kOutput, calls=%fused_computation.2.clone.1 | convolution fusion | flops 270524416 | bytes 689152 | tf_op jit(solution)/shard_map/while/body/eval_jaxpr/dot_general | solution.py:22
  98.2 0.1 reshape.130
  98.3 0.1 reduce_sum.10
  98.5 1.6 %select_reduce_fusion.2 = f32[2048,4]{0,1:T(4,128)S(1)} fusion(pred[4,128]{1,0:T(4,128)(4,1)S(1)} %iota_compare_fusion.2, bf16[2048,128]{1,0:T(8,128)(2,1)S(1)} %get-tuple-element.109, bf16[16,512,128]{2,1,0:T(8,128)(2,1)} %get-tuple-element.108, s32[]{:T(128)} %get-tuple-element.98), kind=kOutput, calls=%fused_computation.2.clone.1 | convolution fusion | flops 270524416 | bytes 689152 | tf_op jit(solution)/shard_map/while/body/eval_jaxpr/dot_general | solution.py:22
  100.2 0.1 reshape.130
  100.3 0.1 reduce_sum.10
  100.5 1.6 %select_reduce_fusion.2 = f32[2048,4]{0,1:T(4,128)S(1)} fusion(pred[4,128]{1,0:T(4,128)(4,1)S(1)} %iota_compare_fusion.2, bf16[2048,128]{1,0:T(8,128)(2,1)S(1)} %get-tuple-element.109, bf16[16,512,128]{2,1,0:T(8,128)(2,1)} %get-tuple-element.108, s32[]{:T(128)} %get-tuple-element.98), kind=kOutput, calls=%fused_computation.2.clone.1 | convolution fusion | flops 270524416 | bytes 689152 | tf_op jit(solution)/shard_map/while/body/eval_jaxpr/dot_general | solution.py:22
  102.2 0.1 reshape.130
  102.2 0.1 reduce_sum.10
  102.5 1.6 %select_reduce_fusion.2 = f32[2048,4]{0,1:T(4,128)S(1)} fusion(pred[4,128]{1,0:T(4,128)(4,1)S(1)} %iota_compare_fusion.2, bf16[2048,128]{1,0:T(8,128)(2,1)S(1)} %get-tuple-element.109, bf16[16,512,128]{2,1,0:T(8,128)(2,1)} %get-tuple-element.108, s32[]{:T(128)} %get-tuple-element.98), kind=kOutput, calls=%fused_computation.2.clone.1 | convolution fusion | flops 270524416 | bytes 689152 | tf_op jit(solution)/shard_map/while/body/eval_jaxpr/dot_general | solution.py:22
  104.1 0.1 reshape.130
  104.2 0.1 reduce_sum.10
  104.4 0.3 fusion.7
  106.2 0.7 reshape.127
  106.8 3.9 %all-to-all-start = ((f32[16,1,256]{2,1,0:T(1,128)}), f32[16,1,256]{2,1,0:T(1,128)S(1)}, u32[]{:S(2)}, u32[]{:S(2)}) async-start(f32[16,1,256]{2,1,0:T(1,128)} %reshape.127), calls=%async_computation | async-start | bytes 32768 | tf_op jit(solution)/shard_map/all_to_all | solution.py:37
  110.8 4.5 %gather_fusion = s32[1024]{0:T(1024)S(1)} fusion(s32[1024]{0:T(1024)S(1)} %copy-done, s32[1024]{0:T(1024)S(1)} %broadcast_clamp_fusion), kind=kCustom, calls=%fused_computation | custom fusion | bytes 12288 | tf_op jit(solution)/shard_map/jit(_take)/gather | solution.py:40
  115.4 7.5 %all-to-all-done = f32[16,1,256]{2,1,0:T(1,128)S(1)} async-done(((f32[16,1,256]{2,1,0:T(1,128)}), f32[16,1,256]{2,1,0:T(1,128)S(1)}, u32[]{:S(2)}, u32[]{:S(2)}) %all-to-all-start) | async-done | bytes 16416 | tf_op jit(solution)/shard_map/all_to_all | solution.py:37
  122.9 0.5 broadcast.70
  123.4 0.7 reduce
  124.1 0.1 reshape.128
  124.2 0.2 copy.75
  124.4 7.3 %gather_fusion.1 = f32[1024]{0:T(1024)S(1)} fusion(f32[4,1024]{0,1:T(8,128)S(1)} %bitcast.59, s32[1024]{0:T(1024)S(1)} %bitcast.58), kind=kCustom, calls=%fused_computation.1 | custom fusion | bytes 16384 | tf_op jit(solution)/shard_map/jit(take_along_axis)/gather | solution.py:40
  131.8 1.9 %sort_prefixfusion = f32[4,10]{1,0:T(4,128)} fusion(f32[4,256]{1,0:T(4,128)S(1)} %and_select_fusion), kind=kCustom, calls=%top_k.9.sort_prefix | custom fusion | flops 10240 | bytes 4256 | tf_op jit(solution)/shard_map/top_k | solution.py:41
  (93 shorter events, 2.8 us)
Async XLA Ops:
  0.6 110.2 %copy-start = (s32[1024]{0:T(1024)S(1)}, s32[1024]{0:T(1024)}, u32[]{:S(2)}) copy-start(s32[1024]{0:T(1024)} %param.10) | copy-start | bytes 12292
  72.7 38.1 %copy-start.1 = (s32[4,256]{1,0:T(4,128)S(1)}, s32[4,256]{1,0:T(4,128)}, u32[]{:S(2)}) copy-start(s32[4,256]{1,0:T(4,128)} %param.11) | copy-start | bytes 12292
  106.8 16.0 %all-to-all-start = ((f32[16,1,256]{2,1,0:T(1,128)}), f32[16,1,256]{2,1,0:T(1,128)S(1)}, u32[]{:S(2)}, u32[]{:S(2)}) async-start(f32[16,1,256]{2,1,0:T(1,128)} %reshape.127), calls=%async_computation | async-start | bytes 32768 | tf_op jit(solution)/shard_map/all_to_all | solution.py:37
  131.7 1.9 %copy-start.2 = (f32[4,256]{1,0:T(4,128)}, f32[4,256]{1,0:T(4,128)S(1)}, u32[]{:S(2)}) copy-start(f32[4,256]{1,0:T(4,128)S(1)} %and_select_fusion) | copy-start | bytes 12292
